TPU v7x, 32 devices: a whole 2x2x4 slice. The times are simulated.
32 devices in a mesh: var: 4 (over z), lat: 4 (over x, core), lon: 2 (over y).
Axes of the slice: x: 2, y: 2, z: 4, core: 2. Of those that a mesh axis runs over, the one named last changes fastest.
Arguments:
- state: bfloat16 [1, 256, 384, 1024], P(None, 'var', 'lat', 'lon'), may hold values from -6 to 6
- weights_in: bfloat16 [2, 256, 256], replicated, may hold values from -0.25 to 0.25
- bias_in: float32 [2, 256], replicated, may hold values from -3 to 3
- weights_out: bfloat16 [2, 256, 256], replicated, may hold values from -2 to 2
Outputs:
- field: bfloat16 [1, 256, 384, 1024], P(None, 'var', 'lat', 'lon')
- zonal: float32 [1, 256, 384], P(None, 'var', 'lat')
- energy: float32 [256], P('var')
All inputs are finite; a program needn't handle non-finite values.
Results may differ from a plain program's by a relative error of at most 0.012.
Values may be sent and summed in bfloat16 or wider, within the bound.
A program may use at most 64 MiB of HBM per device.

v0:
```python
import math

import jax
import jax.numpy as jnp
from jax import lax
from jax.sharding import PartitionSpec as P

LAT = 384
LON = 1024
MLAT = 96
MLON = 96


def lon_forward(first, count):
    index = first + jnp.arange(count, dtype=jnp.int32)
    modes = jnp.arange(MLON, dtype=jnp.int32)
    phase = index[:, None] * modes[None, :] % LON
    angle = phase.astype(jnp.float32) * (2.0 * math.pi / LON)
    scale = 1.0 / math.sqrt(LAT * LON)
    return (jnp.stack([jnp.cos(angle), -jnp.sin(angle)], 1) * scale).astype(jnp.bfloat16)


def lat_forward(first, count):
    freqs = jnp.arange(MLAT, dtype=jnp.int32) - MLAT // 2
    index = first + jnp.arange(count, dtype=jnp.int32)
    phase = jnp.mod(freqs[:, None] * index[None, :], LAT)
    angle = phase.astype(jnp.float32) * (2.0 * math.pi / LAT)
    cosine, sine = (jnp.cos(angle), jnp.sin(angle))
    return jnp.stack([jnp.stack([cosine, sine]), jnp.stack([-sine, cosine])])


def lat_inverse(first, count):
    freqs = jnp.arange(MLAT, dtype=jnp.int32) - MLAT // 2
    index = first + jnp.arange(count, dtype=jnp.int32)
    phase = jnp.mod(index[:, None] * freqs[None, :], LAT)
    angle = phase.astype(jnp.float32) * (2.0 * math.pi / LAT)
    cosine, sine = (jnp.cos(angle), jnp.sin(angle))
    return jnp.stack([jnp.stack([cosine, -sine]), jnp.stack([sine, cosine])]).astype(jnp.bfloat16)


def lon_inverse(first, count):
    modes = jnp.arange(MLON, dtype=jnp.int32)
    index = first + jnp.arange(count, dtype=jnp.int32)
    phase = modes[:, None] * index[None, :] % LON
    angle = phase.astype(jnp.float32) * (2.0 * math.pi / LON)
    factor = jnp.where(modes == 0, 1.0, 2.0).astype(jnp.float32)[:, None] / math.sqrt(LAT * LON)
    return jnp.stack([factor * jnp.cos(angle), -factor * jnp.sin(angle)]).astype(jnp.bfloat16)


def area_weights(first, count):
    index = first + jnp.arange(count, dtype=jnp.int32)
    return jnp.cos(math.pi * ((index.astype(jnp.float32) + 0.5) / LAT - 0.5))


def complex_block(pair):
    real_part, imag_part = (pair[0], pair[1])
    return jnp.stack(
        [jnp.stack([real_part, -imag_part], 1), jnp.stack([imag_part, real_part], 1)], 0
    )


def body(state, weights_in, bias_in, weights_out):
    batch, cdev, latdev, londev = state.shape
    nlat = lax.axis_size("lat")
    nlon = lax.axis_size("lon")
    lat_first = lax.axis_index("lat") * latdev
    lon_first = lax.axis_index("lon") * londev
    modes_lat = MLAT // nlat
    modes_lon = MLON // nlon
    qtab = lat_forward(lat_first, latdev)
    qsplit = qtab.reshape(2, 2, nlat, modes_lat, latdev)
    lonpart = jnp.einsum(
        "bcnl,lpk->pbcnk", state, lon_forward(lon_first, londev), preferred_element_type=jnp.float32
    )
    lonsplit = lonpart.reshape(2, batch, cdev, latdev, nlon, modes_lon)
    partial_value = jnp.einsum(
        "qpIJn,pbcnKk->qbcIKJk", qsplit, lonsplit, precision=lax.Precision.HIGHEST
    )
    spectrum = lax.psum_scatter(
        partial_value.reshape(2, batch, cdev, -1), ("lat", "lon"), scatter_dimension=3, tiled=True
    )
    spectrum = spectrum.astype(jnp.bfloat16)
    block_in = complex_block(weights_in)
    block_out = complex_block(weights_out)
    whole = lax.all_gather(spectrum, "var", axis=2, tiled=True)
    owned = lax.dynamic_slice_in_dim(block_out, lax.axis_index("var") * cdev, cdev, 1)
    hidden = jnp.einsum("qhpc,pbcj->qbhj", block_in, whole, preferred_element_type=jnp.float32)
    hidden = jnp.maximum(hidden + bias_in[:, None, :, None], 0.0).astype(jnp.bfloat16)
    mixed = jnp.einsum("qoph,pbhj->qboj", owned, hidden, preferred_element_type=jnp.float32).astype(
        jnp.bfloat16
    )
    mixed = mixed.reshape(2, batch, cdev, modes_lat, modes_lon)
    rtab = lat_inverse(lat_first, latdev)
    table = rtab
    latback = jnp.einsum(
        "qpnj,pbcjk->qbcnk",
        table,
        lax.all_gather(mixed, "lat", axis=3, tiled=True),
        preferred_element_type=jnp.float32,
    ).astype(jnp.bfloat16)
    htab = lon_inverse(lon_first, londev)
    table = htab
    result = jnp.einsum(
        "pbcnk,pkl->bcnl",
        lax.all_gather(latback, "lon", axis=4, tiled=True),
        table,
        preferred_element_type=jnp.float32,
    )
    active = jax.nn.gelu(result, approximate=False)
    field = active.astype(jnp.bfloat16)
    weights = area_weights(lat_first, latdev)
    denominator = batch * LON * jnp.sum(area_weights(0, LAT))
    row_total = jnp.sum(active, -1)
    row_square = jnp.sum(active * active, -1)
    summed, squared = lax.psum((row_total, row_square), "lon")
    zonal = summed / LON
    local = jnp.sum(squared * weights[None, None, :], axis=(0, 2))
    energy = lax.psum(local, "lat") / denominator
    return (field, zonal, energy)


def solution(mesh):
    return jax.shard_map(
        body,
        mesh=mesh,
        in_specs=(P(None, "var", "lat", "lon"), P(), P(), P()),
        out_specs=(P(None, "var", "lat", "lon"), P(None, "var", "lat"), P("var")),
        check_vma=False,
    )
```

profile of v0, /device:TPU:25, one launch (start us, length us, event | category | flops | bytes accessed | tf_op | source)
XLA Modules:
  0.0 284.5 jit_solution(11124718657220605227)
XLA Ops:
  7.2 0.0 reduce-scatter.2.cloned.1.call-start
  7.2 0.8 fusion.71
  8.1 0.3 fusion.82
  8.3 4.4 %fusion.15 = f32[2,96,64,96]{3,1,2,0:T(8,128)S(1)} fusion(bf16[1,64,96,512]{3,2,1,0:T(8,128)(2,1)} %param.4, f32[512,1,96]{0,2,1:T(8,128)S(1)} %get-tuple-element.24, f32[512,1,96]{0,2,1:T(8,128)S(1)} %get-tuple-element.23), kind=kOutput, calls=%fused_computation.25 | convolution fusion | flops 1208254464 | bytes 11403264 | tf_op jit(solution)/shard_map/bcnl,lpk->pbcnk/dot_general | solution.py:72
  12.8 12.8 %fusion.17 = f32[2,1,64,4,2,24,48]{2,5,3,0,6,4,1:T(8,128)} fusion(f32[2,64,96,2,48,1,1]{2,4,3,1,0,6,5:T(8,128)S(1)} %bitcast.169, f32[1,1,4,24,96]{4,3,1,2,0:T(8,128)S(1)} %get-tuple-element.20, f32[1,1,4,24,96]{4,3,1,2,0:T(8,128)S(1)} %get-tuple-element.19, f32[1,1,4,24,96]{4,3,1,2,0:T(8,128)S(1)} %get-tuple-element.18), kind=kOutput, calls=%fused_computation.28 | convolution fusion | flops 2718019584 | bytes 9547776 | tf_op jit(solution)/shard_map/qpIJn,pbcnKk->qbcIKJk/dot_general | solution.py:76
  25.6 12.4 %copy.27 = f32[2,1,64,4,2,24,48]{6,5,4,3,2,0,1:T(8,128)} copy(f32[2,1,64,4,2,24,48]{2,5,3,0,6,4,1:T(8,128)} %fusion.17) | data formatting | bytes 9437184 | tf_op jit(solution)/shard_map/qpIJn,pbcnKk->qbcIKJk/transpose | solution.py:76
  38.0 0.0 copy-start
  38.0 0.0 copy-start.1
  38.0 0.0 copy-start.2
  38.0 13.1 %reshape.714 = f32[2,1,64,9216]{3,2,0,1:T(8,128)} reshape(f32[2,1,64,4,2,24,48]{6,5,4,3,2,0,1:T(8,128)} %copy.27) | data formatting | bytes 9437184 | tf_op jit(solution)/shard_map/reshape | solution.py:80
  51.1 0.0 reduce-scatter.2.cloned.1.call-update
  51.1 0.0 all-gather.4.cloned.1.call-start
  51.2 54.7 %reduce-scatter.2.cloned.1.call-done = f32[2,1,64,1152]{3,2,0,1:T(8,128)} async-done(((f32[2,1,64,9216]{3,2,0,1:T(8,128)}), f32[2,1,64,1152]{3,2,0,1:T(8,128)}) %reduce-scatter.2.cloned.1.call-update) | async-done | bytes 589840 | tf_op jit(solution)/shard_map/reduce_scatter | solution.py:79
  105.9 1.1 convert_element_type.119
  107.0 1.0 copy.28
  108.0 0.0 all-gather.4.cloned.1.call-update
  108.0 0.2 all-gather.6.cloned.1.call-start
  108.3 0.0 copy-done
  108.3 0.0 copy-done.1
  108.4 0.1 maximum_bitcast_fusion
  108.5 28.3 %all-gather.4.cloned.1.call-done = bf16[2,1,256,1152]{3,0,1,2:T(2,128)(2,1)} async-done(((bf16[2,1,64,1152]{3,0,1,2:T(2,128)(2,1)}), bf16[2,1,256,1152]{3,0,1,2:T(2,128)(2,1)}) %all-gather.4.cloned.1.call-update) | async-done | bytes 1179664 | tf_op jit(solution)/shard_map/all_gather | solution.py:85
  136.8 3.5 %copy.29 = bf16[2,1,256,1152]{2,3,0,1:T(8,128)(2,1)S(1)} copy(bf16[2,1,256,1152]{3,0,1,2:T(2,128)(2,1)} %all-gather.4.cloned.1.call-done) | data formatting | bytes 2359296 | tf_op jit(solution)/shard_map/all_gather | solution.py:85
  140.3 0.0 copy-done.2
  140.3 1.1 fusion.28
  141.4 0.7 reshape.717
  142.2 1.3 copy.31
  143.5 0.0 all-gather.6.cloned.1.call-update
  143.5 0.0 all-gather.8.cloned.1.call-start
  143.5 0.3 negate_convert_fusion
  143.9 25.2 %all-gather.6.cloned.1.call-done = bf16[2,1,64,96,48]{2,4,1,0,3:T(8,128)(2,1)} async-done(((bf16[2,1,64,24,48]{2,4,1,0,3:T(8,128)(2,1)}), bf16[2,1,64,96,48]{2,4,1,0,3:T(8,128)(2,1)}) %all-gather.6.cloned.1.call-update) | async-done | bytes 1179664 | tf_op jit(solution)/shard_map/all_gather | solution.py:98
  169.1 4.4 %fusion.31 = bf16[2,1,64,96,48]{3,2,1,0,4:T(8,128)(2,1)} fusion(bf16[2,64,96,48,1]{1,3,0,2,4:T(8,128)(2,1)} %bitcast.170, bf16[1,2,96,96]{3,2,1,0:T(8,128)(2,1)S(1)} %get-tuple-element.17, bf16[1,2,96,96]{3,2,1,0:T(8,128)(2,1)S(1)} %get-tuple-element.16), kind=kOutput, calls=%fused_computation.41 | convolution fusion | flops 227229696 | bytes 2433024 | tf_op jit(solution)/shard_map/qpnj,pbcjk->qbcnk/dot_general | solution.py:95
  173.5 0.0 all-gather.8.cloned.1.call-update
  173.5 0.6 cosine_reduce_fusion
  174.8 0.1 multiply_cosine_fusion
  174.9 0.8 multiply_convert_fusion.1
  175.7 42.3 %all-gather.8.cloned.1.call-done = bf16[2,1,64,96,96]{3,2,1,0,4:T(8,128)(2,1)} async-done(((bf16[2,1,64,96,48]{3,2,1,0,4:T(8,128)(2,1)}), bf16[2,1,64,96,96]{3,2,1,0,4:T(8,128)(2,1)}) %all-gather.8.cloned.1.call-update) | async-done | bytes 2359312 | tf_op jit(solution)/shard_map/all_gather | solution.py:105
  218.0 4.8 %copy.34 = bf16[2,1,64,96,96]{4,3,0,2,1:T(8,128)(2,1)S(1)} copy(bf16[2,1,64,96,96]{3,2,1,0,4:T(8,128)(2,1)} %all-gather.8.cloned.1.call-done) | data formatting | bytes 4718592 | tf_op jit(solution)/shard_map/all_gather | solution.py:105
  222.8 40.2 %multiply_reduce_fusion = (f32[64,96]{1,0:T(8,128)S(1)}, f32[64,96]{1,0:T(8,128)S(1)}, bf16[1,64,96,512]{3,2,1,0:T(8,128)(2,1)}) fusion(bf16[1,96,512]{2,1,0:T(8,128)(2,1)S(1)} %get-tuple-element.22, bf16[1,96,512]{2,1,0:T(8,128)(2,1)S(1)} %get-tuple-element.21, bf16[2,1,64,96,96]{4,3,0,2,1:T(8,128)(2,1)S(1)} %copy.34), kind=kOutput, calls=%fused_computation.6 | convolution fusion | flops 1421955072 | bytes 8896512 | tf_op jit(solution)/shard_map/pbcnk,pkl->bcnl/dot_general | solution.py:103
  263.0 6.0 %all-reduce = (f32[1,64,96]{2,1,0:T(8,128)S(1)}, f32[1,64,96]{2,1,0:T(8,128)S(1)}) all-reduce(f32[1,64,96]{2,1,0:T(8,128)S(1)} %bitcast.172, f32[1,64,96]{2,1,0:T(8,128)S(1)} %bitcast.171), channel_id=1, replica_groups=mesh['var'=4,'lat'=4,'lon'=2] {'lon'}, use_global_device_ids=true, to_apply=%region_2.3 | all-reduce | flops 12288 | bytes 98304 | tf_op jit(solution)/shard_map/psum | solution.py:115
  269.0 0.6 broadcast_multiply_fusion
  269.6 0.1 multiply_reduce_fusion.1
  269.7 7.7 %psum.23 = f32[64]{0:T(128)S(1)} all-reduce(f32[64]{0:T(128)S(1)} %multiply_reduce_fusion.1), channel_id=1, replica_groups=mesh['var'=4,'lat'=4,'lon'=2] {'lat'}, use_global_device_ids=true, to_apply=%region_6.7 | all-reduce | flops 64 | bytes 512 | tf_op jit(solution)/shard_map/psum | solution.py:118
  277.4 0.5 broadcast_divide_fusion
  (9 shorter events, 0.1 us)
Async XLA Ops:
  7.2 98.7 %reduce-scatter.2.cloned.1.call-start = ((), (), s32[]{:S(2)}) async-start(), calls=%async_computation.1 | async-start | bytes 5308416 | tf_op jit(solution)/shard_map/reduce_scatter | solution.py:79
  38.0 70.3 %copy-start = (bf16[2,256,256]{2,1,0:T(8,128)(2,1)S(1)}, bf16[2,256,256]{2,1,0:T(8,128)(2,1)}, u32[]{:S(2)}) copy-start(bf16[2,256,256]{2,1,0:T(8,128)(2,1)} %param.5) | copy-start | bytes 786436
  38.0 70.3 %copy-start.1 = (bf16[2,256,256]{2,1,0:T(8,128)(2,1)S(1)}, bf16[2,256,256]{2,1,0:T(8,128)(2,1)}, u32[]{:S(2)}) copy-start(bf16[2,256,256]{2,1,0:T(8,128)(2,1)} %param.7) | copy-start | bytes 786436
  38.0 102.3 %copy-start.2 = (f32[2,256]{1,0:T(2,128)S(1)}, f32[2,256]{1,0:T(2,128)}, u32[]{:S(2)}) copy-start(f32[2,256]{1,0:T(2,128)} %param.6) | copy-start | bytes 6148
  51.1 85.7 %all-gather.4.cloned.1.call-start = ((), (), s32[]{:S(2)}) async-start(), calls=%async_computation.2 | async-start | bytes 1474560 | tf_op jit(solution)/shard_map/all_gather | solution.py:85
  108.0 61.1 %all-gather.6.cloned.1.call-start = ((), (), s32[]{:S(2)}) async-start(), calls=%async_computation.3 | async-start | bytes 2949120 | tf_op jit(solution)/shard_map/all_gather | solution.py:98
  143.5 74.5 %all-gather.8.cloned.1.call-start = ((), (), s32[]{:S(2)}) async-start(), calls=%async_computation.4 | async-start | bytes 4718592 | tf_op jit(solution)/shard_map/all_gather | solution.py:105
Sparse Core Ops, SparseCore 0:
  51.3 54.5 reduce-scatter.1
  108.1 28.6 all-gather.3
  143.6 25.4 all-gather.5
  173.6 44.3 all-gather.7
where the time goes:
time: 287 us; the launch traced here: 284 us
  waiting for transfers between devices  151 us (53%)
  matrix products  62.9 us (22%)
  local copies, waits for them, and re-layouts  36.8 us (13%)
  between operations  14.6 us (5%)
  blocking collectives  13.7 us (5%)
  other arithmetic  5.38 us (2%)
    reduce_scatter x1, waiting for transfers between devices, body(): lax.psum_scatter(partial_value.reshape(2, batch, cdev, -1), ('lat', 'lon'...  54.7 us
    all_gather x1, waiting for transfers between devices, body(): lax.all_gather(latback, 'lon', axis=4, tiled=True)  42.3 us
    dot_general x1, matrix products, body(): jnp.einsum('pbcnk,pkl->bcnl', lax.all_gather(latback, 'lon', axis=4, tile...  40.2 us
    all_gather x1, waiting for transfers between devices, body(): whole = lax.all_gather(spectrum, 'var', axis=2, tiled=True)  28.3 us
    all_gather x1, waiting for transfers between devices, body(): lax.all_gather(mixed, 'lat', axis=3, tiled=True)  25.2 us
    reshape x1, local copies, waits for them, and re-layouts, body(): partial_value.reshape(2, batch, cdev, -1)  13.1 us
    dot_general x1, matrix products, body(): jnp.einsum('qpIJn,pbcnKk->qbcIKJk', qsplit, lonsplit, precision=lax.Preci...  12.8 us
    transpose x1, local copies, waits for them, and re-layouts, body(): jnp.einsum('qpIJn,pbcnKk->qbcIKJk', qsplit, lonsplit, precision=lax.Preci...  12.4 us
  transfers between devices with their start and end apart: 4, of which 4 were waited for; matrix products, arithmetic and copies ran while one was open for 1% of the time, Pallas kernels for 0%

commit v1 on v0

--- a/solution.py
+++ b/solution.py
@@ -1,8 +1,11 @@
+import functools
 import math
 
 import jax
 import jax.numpy as jnp
 from jax import lax
+from jax.experimental import pallas as pl
+from jax.experimental.pallas import tpu as pltpu
 from jax.sharding import PartitionSpec as P
 
 LAT = 384
@@ -59,7 +62,7 @@
     )
 
 
-def body(state, weights_in, bias_in, weights_out):
+def plain_body(state, weights_in, bias_in, weights_out):
     batch, cdev, latdev, londev = state.shape
     nlat = lax.axis_size("lat")
     nlon = lax.axis_size("lon")
@@ -118,8 +121,322 @@
     energy = lax.psum(local, "lat") / denominator
     return (field, zonal, energy)
 
+LANES = 128
+MESH = pl.DeviceIdType.MESH
+
+
+def pad_lanes(table):
+    return jnp.pad(table, [(0, 0)] * (table.ndim - 1) + [(0, LANES - table.shape[-1])])
+
+
+def forward_kernel(x_ref, e_ref, q_ref, out_ref):
+    channels, rows, count = x_ref.shape
+    lon = jnp.dot(
+        x_ref[...].reshape(channels * rows, count), e_ref[...], preferred_element_type=jnp.float32
+    ).astype(jnp.bfloat16)
+    lon = lon.reshape(channels, rows, 2 * LANES)
+    parts = []
+    for c in range(channels):
+        both = jnp.concatenate([lon[c, :, :LANES], lon[c, :, LANES:]], 0)
+        parts.append(jnp.dot(q_ref[...], both, preferred_element_type=jnp.float32))
+    out_ref[...] = jnp.swapaxes(jnp.stack(parts), 0, 1).astype(jnp.bfloat16)
+
+
+def inverse_kernel(g_ref, r_ref, h_ref, field_ref, zonal_ref, square_ref):
+    channels = g_ref.shape[1]
+    rows = field_ref.shape[1]
+    modes = jnp.swapaxes(g_ref[...].astype(jnp.float32), 0, 1).astype(jnp.bfloat16)
+    for c in range(channels):
+        lat = jnp.dot(r_ref[...], modes[c], preferred_element_type=jnp.float32).astype(jnp.bfloat16)
+        both = jnp.concatenate([lat[:rows], lat[rows:]], 1)
+        result = jnp.dot(both, h_ref[...], preferred_element_type=jnp.float32)
+        active = (0.5 * result) * (1.0 + lax.erf(result * math.sqrt(0.5)))
+        field_ref[c] = active.astype(jnp.bfloat16)
+        zonal_ref[c, :] = jnp.sum(active, -1)
+        square_ref[c, :] = jnp.sum(active * active, -1)
+
+
+def exchange_kernel(
+    sizes, p_ref, win_ref, bias_ref, wout_ref, out_ref,
+    pair, sums, slots, spec, gathered, back,
+    s_pair, r_pair, s_red, r_red, s_z, r_z, s_b, r_b, s_all, r_all, s_fwd, r_fwd,
+):
+    nvar, nlat, nlon = sizes
+    v, lat, lon = lax.axis_index("var"), lax.axis_index("lat"), lax.axis_index("lon")
+    upper, core = lat // 2, lax.rem(lat, 2)
+    nupper = nlat // 2
+    block = p_ref.shape[0] // (nlat * nlon)
+    part = block // nvar
+    offsets = [(a, b) for a in range(nupper) for b in range(nlon)]
+    count = len(offsets)
+
+    def chip(t, sign=1):
+        a, b = offsets[t]
+        return (
+            lax.rem(upper + sign * a + nupper, nupper),
+            lax.rem(lon + sign * b + nlon, nlon),
+        )
+
+    def rows(where, parity):
+        a, b = where
+        return pl.ds(((a * 2 + parity) * nlon + b) * block, block)
+
+    def send(src, dst, ssem, rsem, target):
+        return pltpu.make_async_remote_copy(
+            src_ref=src, dst_ref=dst, send_sem=ssem, recv_sem=rsem,
+            device_id=target, device_id_type=MESH,
+        )
+
+    sibling = {"lat": upper * 2 + 1 - core}
+
+    def peer(t):
+        a, b = chip(t)
+        return {"lat": a * 2 + core, "lon": b}
+
+    def other(d):
+        return {"var": lax.rem(v + d, nvar)}
+
+    barrier = pltpu.get_barrier_semaphore()
+    targets = [sibling] + [peer(t) for t in range(1, count)] + [other(d) for d in range(1, nvar)]
+    for target in targets:
+        pl.semaphore_signal(barrier, inc=1, device_id=target, device_id_type=MESH)
+    pl.semaphore_wait(barrier, len(targets))
+
+    order = list(range(1, count))[::-1] + [0]
+    pairs = {}
+    for t in order:
+        pairs[t] = send(
+            p_ref.at[rows(chip(t), 1 - core)], pair.at[t], s_pair.at[t], r_pair.at[t], sibling
+        )
+        pairs[t].start()
+    reds = {}
+    for t in order:
+        pairs[t].wait_recv()
+        mine = p_ref[rows(chip(t), core)].astype(jnp.float32) + pair[t].astype(jnp.float32)
+        sums[t] = mine.astype(jnp.bfloat16)
+        if t:
+            reds[t] = send(sums.at[t], slots.at[t - 1], s_red.at[t - 1], r_red.at[t - 1], peer(t))
+            reds[t].start()
+    for t in order[:-1]:
+        reds[t].wait_recv()
+    total = sums[0].astype(jnp.float32)
+    for t in range(1, count):
+        total = total + slots[t - 1].astype(jnp.float32)
+    spec[...] = total.astype(jnp.bfloat16)
+    zs = []
+    for d in range(1, nvar):
+        copy = send(
+            spec.at[pl.ds(lax.rem(v + d, nvar) * part, part)], gathered.at[v],
+            s_z.at[d - 1], r_z.at[d - 1], other(d),
+        )
+        copy.start()
+        zs.append(copy)
+    gathered[v] = spec[pl.ds(v * part, part)]
+    for d in range(1, nvar):
+        src = gathered.at[lax.rem(v - d + nvar, nvar)]
+        send(src, src, s_z.at[d - 1], r_z.at[d - 1], other(d)).wait_recv()
+    held = gathered[...]
+    cdev = held.shape[2]
+    cols = []
+    for j in range(part // 2):
+        cols.append(held[:, 2 * j : 2 * j + 2].reshape(nvar * 2 * cdev, LANES))
+    spectrum = jnp.concatenate(cols, 1)
+    hidden = jnp.dot(win_ref[...], spectrum, preferred_element_type=jnp.float32)
+    hidden = jnp.maximum(hidden + bias_ref[...], 0.0).astype(jnp.bfloat16)
+    mixed = jnp.dot(wout_ref[...], hidden, preferred_element_type=jnp.float32).astype(jnp.bfloat16)
+    for j in range(part // 2):
+        back[:, 2 * j : 2 * j + 2] = mixed[:, j * LANES : (j + 1) * LANES].reshape(nvar, 2, cdev, LANES)
+    base = (lat * nlon + lon) * block
+    bs = []
+    for d in range(1, nvar):
+        copy = send(
+            back.at[lax.rem(v + d, nvar)], out_ref.at[pl.ds(base + v * part, part)],
+            s_b.at[d - 1], r_b.at[d - 1], other(d),
+        )
+        copy.start()
+        bs.append(copy)
+    out_ref[pl.ds(base + v * part, part)] = back[v]
+    for d in range(1, nvar):
+        src = out_ref.at[pl.ds(base + lax.rem(v - d + nvar, nvar) * part, part)]
+        send(src, src, s_b.at[d - 1], r_b.at[d - 1], other(d)).wait_recv()
+    own = out_ref.at[pl.ds(base, block)]
+    alls = []
+    for t in order[:-1]:
+        copy = send(own, own, s_all.at[t - 1], r_all.at[t - 1], peer(t))
+        copy.start()
+        alls.append(copy)
+    fwd = [send(own, own, s_fwd.at[0], r_fwd.at[0], sibling)]
+    fwd[0].start()
+    for t in range(1, count):
+        got = out_ref.at[rows(chip(t, -1), core)]
+        send(got, got, s_all.at[t - 1], r_all.at[t - 1], peer(t)).wait_recv()
+        copy = send(got, got, s_fwd.at[t], r_fwd.at[t], sibling)
+        copy.start()
+        fwd.append(copy)
+    for t in range(count):
+        got = out_ref.at[rows(chip(t, -1), 1 - core)]
+        send(got, got, s_fwd.at[t], r_fwd.at[t], sibling).wait_recv()
+    for copy in list(pairs.values()) + list(reds.values()) + zs + bs + alls + fwd:
+        copy.wait_send()
+
+
+def statistics_kernel(sizes, x_ref, zonal_ref, energy_ref, slots, s_sem, r_sem):
+    nvar, nlat, nlon = sizes
+    lat, lon = lax.axis_index("lat"), lax.axis_index("lon")
+    offsets = [(a, b) for a in range(nlat) for b in range(nlon)][1:]
+
+    def target(t):
+        a, b = offsets[t]
+        return {"lat": lax.rem(lat + a, nlat), "lon": lax.rem(lon + b, nlon)}
+
+    barrier = pltpu.get_barrier_semaphore()
+    for t in range(len(offsets)):
+        pl.semaphore_signal(barrier, inc=1, device_id=target(t), device_id_type=MESH)
+    pl.semaphore_wait(barrier, len(offsets))
+    copies = []
+    for t in range(len(offsets)):
+        copy = pltpu.make_async_remote_copy(
+            src_ref=x_ref, dst_ref=slots.at[t], send_sem=s_sem.at[t], recv_sem=r_sem.at[t],
+            device_id=target(t), device_id_type=MESH,
+        )
+        copy.start()
+        copies.append(copy)
+    zonal = x_ref[...]
+    energy = x_ref[...]
+    for t, (a, _) in enumerate(offsets):
+        copies[t].wait_recv()
+        energy = energy + slots[t]
+        if a == 0:
+            zonal = zonal + slots[t]
+    zonal_ref[...] = zonal
+    energy_ref[...] = energy
+    for copy in copies:
+        copy.wait_send()
+
+
+def kernel_body(sizes, state, weights_in, bias_in, weights_out):
+    nvar, nlat, nlon = sizes
+    batch, cdev, latdev, londev = state.shape
+    lat_first = lax.axis_index("lat") * latdev
+    lon_first = lax.axis_index("lon") * londev
+    vmem = pl.BlockSpec(memory_space=pltpu.VMEM)
+    step = 16
+    bf16 = jnp.bfloat16
+    etab = pad_lanes(lon_forward(lon_first, londev)).reshape(londev, 2 * LANES)
+    qtab = lat_forward(lat_first, latdev).astype(bf16)
+    qtab = qtab.transpose(2, 0, 1, 3).reshape(2 * MLAT, 2 * latdev)
+    partial_value = pl.pallas_call(
+        forward_kernel,
+        grid=(cdev // step,),
+        in_specs=[
+            pl.BlockSpec((step, latdev, londev), lambda i: (i, 0, 0)),
+            pl.BlockSpec(etab.shape, lambda i: (0, 0)),
+            pl.BlockSpec(qtab.shape, lambda i: (0, 0)),
+        ],
+        out_specs=pl.BlockSpec((2 * MLAT, step, LANES), lambda i: (0, i, 0)),
+        out_shape=jax.ShapeDtypeStruct((2 * MLAT, cdev, LANES), bf16),
+        compiler_params=pltpu.CompilerParams(vmem_limit_bytes=40 * 2**20),
+        name="forward",
+    )(state[0], etab, qtab)
+
+    hid = weights_in.shape[1]
+    win = complex_block(weights_in).reshape(2, hid, 2, nvar, cdev)
+    win = win.transpose(0, 1, 3, 2, 4).reshape(2 * hid, 2 * nvar * cdev)
+    wout = complex_block(weights_out).reshape(2, nvar, cdev, 2 * hid)
+    wout = wout.transpose(1, 0, 2, 3).reshape(2 * nvar * cdev, 2 * hid)
+    chips = nlat * nlon // 2
+    block = 2 * MLAT // (nlat * nlon)
+    part = block // nvar
+    dma = pltpu.SemaphoreType.DMA
+    whole = pl.pallas_call(
+        functools.partial(exchange_kernel, sizes),
+        in_specs=[vmem] * 4,
+        out_specs=vmem,
+        out_shape=jax.ShapeDtypeStruct(partial_value.shape, bf16),
+        scratch_shapes=[
+            pltpu.VMEM((chips, block, cdev, LANES), bf16),
+            pltpu.VMEM((chips, block, cdev, LANES), bf16),
+            pltpu.VMEM((chips - 1, block, cdev, LANES), bf16),
+            pltpu.VMEM((block, cdev, LANES), bf16),
+            pltpu.VMEM((nvar, part, cdev, LANES), bf16),
+            pltpu.VMEM((nvar, part, cdev, LANES), bf16),
+            dma((chips,)), dma((chips,)),
+            dma((chips - 1,)), dma((chips - 1,)),
+            dma((nvar - 1,)), dma((nvar - 1,)),
+            dma((nvar - 1,)), dma((nvar - 1,)),
+            dma((chips - 1,)), dma((chips - 1,)),
+            dma((chips,)), dma((chips,)),
+        ],
+        compiler_params=pltpu.CompilerParams(
+            collective_id=0, has_side_effects=True, vmem_limit_bytes=40 * 2**20
+        ),
+        name="exchange",
+    )(partial_value, win, bias_in.reshape(2 * hid, 1), wout)
+
+    rtab = lat_inverse(lat_first, latdev)
+    rtab = rtab.transpose(0, 2, 3, 1).reshape(2 * latdev, 2 * MLAT)
+    htab = lon_inverse(lon_first, londev)
+    htab = jnp.pad(htab, ((0, 0), (0, LANES - MLON), (0, 0))).reshape(2 * LANES, londev)
+    field, summed, squared = pl.pallas_call(
+        inverse_kernel,
+        grid=(cdev // step,),
+        in_specs=[
+            pl.BlockSpec((2 * MLAT, step, LANES), lambda i: (0, i, 0)),
+            pl.BlockSpec(rtab.shape, lambda i: (0, 0)),
+            pl.BlockSpec(htab.shape, lambda i: (0, 0)),
+        ],
+        out_specs=[
+            pl.BlockSpec((step, latdev, londev), lambda i: (i, 0, 0)),
+            pl.BlockSpec((step, latdev), lambda i: (i, 0)),
+            pl.BlockSpec((step, latdev), lambda i: (i, 0)),
+        ],
+        out_shape=[
+            jax.ShapeDtypeStruct((cdev, latdev, londev), bf16),
+            jax.ShapeDtypeStruct((cdev, latdev), jnp.float32),
+            jax.ShapeDtypeStruct((cdev, latdev), jnp.float32),
+        ],
+        compiler_params=pltpu.CompilerParams(vmem_limit_bytes=40 * 2**20),
+        name="inverse",
+    )(whole, rtab, htab)
+
+    local = jnp.sum(squared * area_weights(lat_first, latdev)[None, :], axis=1)
+    packed = jnp.concatenate(
+        [summed, jnp.broadcast_to(local[:, None], (cdev, LANES - latdev))], axis=1
+    )
+    zonal, energy = pl.pallas_call(
+        functools.partial(statistics_kernel, sizes),
+        in_specs=[vmem],
+        out_specs=[vmem, vmem],
+        out_shape=[jax.ShapeDtypeStruct((cdev, LANES), jnp.float32)] * 2,
+        scratch_shapes=[
+            pltpu.VMEM((nlat * nlon - 1, cdev, LANES), jnp.float32),
+            dma((nlat * nlon - 1,)), dma((nlat * nlon - 1,)),
+        ],
+        compiler_params=pltpu.CompilerParams(collective_id=1, has_side_effects=True),
+        name="statistics",
+    )(packed)
+    denominator = batch * LON * jnp.sum(area_weights(0, LAT))
+    return (field[None], zonal[None, :, :latdev] / LON, energy[:, latdev] / denominator)
+
 
 def solution(mesh):
+    sizes = tuple(mesh.shape[name] for name in ("var", "lat", "lon"))
+    nvar, nlat, nlon = sizes
+
+    def body(state, weights_in, bias_in, weights_out):
+        batch, cdev, latdev, _ = state.shape
+        fits = (
+            batch == 1
+            and nlat % 2 == 0
+            and MLAT % (nlat * nlon * nvar) == 0
+            and cdev % 16 == 0
+            and latdev < LANES
+            and MLON <= LANES
+        )
+        if fits:
+            return kernel_body(sizes, state, weights_in, bias_in, weights_out)
+        return plain_body(state, weights_in, bias_in, weights_out)
+
     return jax.shard_map(
         body,
         mesh=mesh,

time: 287 us -> 133 us (0.46)
  waiting for transfers between devices: 151 us -> 0 us
  Pallas kernels: 0 us -> 95 us
  matrix products: 62.9 us -> 0 us
  blocking collectives: 13.7 us -> 0 us
  between operations: 14.6 us -> 1.54 us
  local copies, waits for them, and re-layouts: 36.8 us -> 26.2 us
  other arithmetic: 5.38 us -> 10 us
    all_gather x3 -> x0, waiting for transfers between devices: 95.9 us -> none  [the longest x1 42.3 us: body(): lax.all_gather(latback, 'lon', axis=4, tiled=True)]
    pallas_call x0 -> x4, Pallas kernels: none -> 95 us  [the longest x1 65.6 us: kernel_body(): pl.pallas_call(functools.partial(exchange_kernel, sizes), in_specs=[vmem]...]
    dot_general x5 -> x0, matrix products: 62.9 us -> none  [the longest x1 40.2 us: body(): jnp.einsum('pbcnk,pkl->bcnl', lax.all_gather(latback, 'lon', axis=4, tile...]
    reduce_scatter x1 -> x0, waiting for transfers between devices: 54.7 us -> none  [body(): lax.psum_scatter(partial_value.reshape(2, batch, cdev, -1), ('lat', 'lon'...]
    psum x2 -> x0, blocking collectives: 13.7 us -> none  [the longest x1 7.75 us: body(): energy = lax.psum(local, 'lat') / denominator]
    transpose x1 -> x3, local copies, waits for them, and re-layouts: 12.4 us -> 1.03 us  [the longest x1 0.83 us: kernel_body(): wout = wout.transpose(1, 0, 2, 3).reshape(2 * nvar * cdev, 2 * hid)]
    unnamed x6 -> x20, local copies, waits for them, and re-layouts: 0.01 us -> 9.67 us
    all_gather x2 -> x0, local copies, waits for them, and re-layouts: 8.24 us -> none  [the longest x1 4.79 us: body(): lax.all_gather(latback, 'lon', axis=4, tiled=True)]
  transfers between devices with their start and end apart: 4 -> 0, of which waited for: 4 -> 0; matrix products, arithmetic and copies ran while one was open for 1% -> 0% of each run, Pallas kernels for 0% -> 0%
where the time goes in v1:
time: 133 us
  Pallas kernels  95 us (71%)
  local copies, waits for them, and re-layouts  26.2 us (20%)
  other arithmetic  10 us (8%)
  between operations  1.54 us (1%)
    pallas_call x1, Pallas kernels, kernel_body(): pl.pallas_call(functools.partial(exchange_kernel, sizes), in_specs=[vmem]...  65.6 us
    pallas_call x1, Pallas kernels, kernel_body(): pl.pallas_call(inverse_kernel, grid=(cdev // step,), in_specs=[pl.BlockSp...  14.5 us
    unnamed x20, local copies, waits for them, and re-layouts  9.67 us
    pallas_call x1, Pallas kernels, kernel_body(): pl.pallas_call(functools.partial(statistics_kernel, sizes), in_specs=[vme...  7.66 us
    reshape x2, local copies, waits for them, and re-layouts, kernel_body(): win = win.transpose(0, 1, 3, 2, 4).reshape(2 * hid, 2 * nvar * cdev)  7.41 us
    pallas_call x1, Pallas kernels, kernel_body(): pl.pallas_call(forward_kernel, grid=(cdev // step,), in_specs=[pl.BlockSp...  7.19 us
    another operation x2, local copies, waits for them, and re-layouts, complex_block(): jnp.stack([jnp.stack([real_part, -imag_part], 1), jnp.stack([imag_part, r...  2.93 us

profile of v1, /device:TPU:25, one launch (start us, length us, event | category | flops | bytes accessed | tf_op | source)
XLA Modules:
  0.0 132.7 jit_solution(9920602640058573413)
XLA Ops:
  0.7 0.5 negate_convert_fusion
  1.2 0.7 maximum_bitcast_fusion.4
  1.8 0.1 copy.35
  1.9 0.1 reshape.664.q_ref
  2.1 0.8 fusion.16
  2.9 0.1 copy.46.e_ref
  3.1 0.0 copy-start.2
  3.1 2.8 %copy-done.2 = bf16[1,64,96,512]{3,2,1,0:T(8,128)(2,1)S(1)} copy-done((bf16[1,64,96,512]{3,2,1,0:T(8,128)(2,1)S(1)}, bf16[1,64,96,512]{3,2,1,0:T(8,128)(2,1)}, u32[]{:S(2)}) %copy-start.2) | copy-done | bytes 6291480
  5.9 7.2 %forward.1.p_ref = bf16[192,64,128]{2,1,0:T(8,128)(2,1)S(1)} custom-call(bf16[64,96,512]{2,1,0:T(8,128)(2,1)S(1)} %bitcast.37, bf16[512,256]{1,0:T(8,128)(2,1)S(1)} %copy.46.e_ref, bf16[192,192]{1,0:T(8,128)(2,1)S(1)} %reshape.664.q_ref), custom_call_target="tpu_custom_call" | custom-call | tf_op jit(solution)/shard_map/forward/pallas_call | solution.py:328
  13.1 0.0 copy-start.7
  13.1 1.0 slice_bitcast_fusion
  14.1 0.9 fusion.34
  15.0 1.0 copy.39
  16.0 1.8 %stack.100 = bf16[1,4,64,512]{3,2,1,0:T(8,128)(2,1)} reshape(bf16[256,2,256]{2,1,0:T(2,128)(2,1)} %copy.39) | data formatting | bytes 524288 | tf_op jit(solution)/shard_map/stack | solution.py:60
  17.8 1.0 copy.40
  18.8 1.1 stack.102
  19.9 1.0 maximum_bitcast_fusion.1
  20.9 0.8 copy.41
  21.8 1.6 %fusion.35 = (bf16[1,256,256]{2,1,0:T(8,128)(2,1)S(1)}, bf16[1,256,256]{2,1,0:T(8,128)(2,1)}) fusion(bf16[2,256,256]{2,1,0:T(8,128)(2,1)} %param.5), kind=kLoop, calls=%fused_computation.76 | loop fusion | bytes 524288 | tf_op jit(solution)/shard_map/slice | solution.py:59
  23.4 0.1 copy.50
  23.5 1.0 copy.49
  24.5 0.8 maximum_bitcast_fusion
  25.4 3.6 %copy.47 = bf16[2,256,4,2,64]{4,3,2,1,0:T(2,128)(2,1)} copy(bf16[2,256,4,2,64]{1,4,2,3,0:T(8,128)(2,1)} %maximum_bitcast_fusion) | data formatting | bytes 1048576 | tf_op jit(solution)/shard_map/reshape | solution.py:344
  28.9 3.8 %reshape.670.win_ref = bf16[512,512]{1,0:T(8,128)(2,1)} reshape(bf16[2,256,4,2,64]{4,3,2,1,0:T(2,128)(2,1)} %copy.47) | data formatting | bytes 1048576 | tf_op jit(solution)/shard_map/reshape | solution.py:344
  32.8 0.0 copy-done.7
  32.8 0.1 copy.52
  32.9 0.0 copy-start.3
  33.0 1.0 copy-done.3
  34.0 1.0 copy-done.4
  35.0 65.6 %exchange.1.g_ref = bf16[192,64,128]{2,1,0:T(8,128)(2,1)S(1)} custom-call(bf16[192,64,128]{2,1,0:T(8,128)(2,1)S(1)} %forward.1.p_ref, bf16[512,512]{1,0:T(8,128)(2,1)S(1)} %copy-done.3, f32[512,1]{1,0:T(8,128)S(1)} %bitcast.40, bf16[512,512]{1,0:T(8,128)(2,1)S(1)} %bitcast.38), custom_call_target="tpu_custom_call" | custom-call | tf_op jit(solution)/shard_map/exchange/pallas_call | solution.py:351
  100.6 0.0 copy-start
  100.7 1.7 %copy-done = bf16[192,64,128]{2,1,0:T(8,128)(2,1)} copy-done((bf16[192,64,128]{2,1,0:T(8,128)(2,1)}, bf16[192,64,128]{2,1,0:T(8,128)(2,1)S(1)}, u32[]{:S(2)}) %copy-start) | copy-done | bytes 3145752
  102.3 0.0 copy-done.5
  102.3 0.0 copy-done.6
  102.3 0.1 copy.44
  102.5 0.1 reshape.668
  102.6 0.1 copy.45.r_ref
  102.7 0.8 multiply_convert_fusion.1
  103.6 0.0 copy-start.1
  103.6 1.9 %copy-done.1 = bf16[192,64,128]{2,1,0:T(8,128)(2,1)S(1)} copy-done((bf16[192,64,128]{2,1,0:T(8,128)(2,1)S(1)}, bf16[192,64,128]{2,1,0:T(8,128)(2,1)}, u32[]{:S(2)}) %copy-start.1) | copy-done | bytes 3145752
  105.4 14.5 %inverse.1 = (bf16[64,96,512]{2,1,0:T(8,128)(2,1)}, f32[64,96]{1,0:T(8,128)S(1)}, f32[64,96]{1,0:T(8,128)S(1)}) custom-call(bf16[192,64,128]{2,1,0:T(8,128)(2,1)S(1)} %copy-done.1, bf16[192,192]{1,0:T(8,128)(2,1)S(1)} %copy.45.r_ref, bf16[256,512]{1,0:T(8,128)(2,1)S(1)} %bitcast.39), custom_call_target="tpu_custom_call" | custom-call | tf_op jit(solution)/shard_map/inverse/pallas_call | solution.py:380
  120.0 0.1 multiply_reduce_fusion
  120.1 0.1 broadcast_in_dim.15
  120.2 0.7 pad_maximum_fusion.2.x_ref
  120.9 7.7 %statistics.1 = (f32[64,128]{1,0:T(8,128)}, f32[64,128]{1,0:T(8,128)}) custom-call(f32[64,128]{1,0:T(8,128)} %pad_maximum_fusion.2.x_ref), custom_call_target="tpu_custom_call" | custom-call | tf_op jit(solution)/shard_map/statistics/pallas_call | solution.py:406
  128.6 1.4 %multiply_bitcast_fusion = f32[1,64,96]{2,1,0:T(8,128)} fusion(f32[64,128]{1,0:T(8,128)} %get-tuple-element.11), kind=kLoop, calls=%fused_computation.64 | loop fusion | flops 6144 | bytes 49152 | tf_op jit(solution)/shard_map/div | solution.py:419
  129.9 0.6 cosine_reduce_fusion
  131.2 1.5 %fusion.31 = f32[64]{0:T(128)} fusion(f32[64,128]{1,0:T(8,128)} %get-tuple-element.12, f32[]{:T(128)S(6)} %mul.275), kind=kLoop, calls=%fused_computation.66 | loop fusion | flops 64 | bytes 516 | tf_op jit(solution)/shard_map/div | solution.py:419
  (16 shorter events, 0.3 us)
Async XLA Ops:
  3.1 2.8 %copy-start.2 = (bf16[1,64,96,512]{3,2,1,0:T(8,128)(2,1)S(1)}, bf16[1,64,96,512]{3,2,1,0:T(8,128)(2,1)}, u32[]{:S(2)}) copy-start(bf16[1,64,96,512]{3,2,1,0:T(8,128)(2,1)} %param.4) | copy-start | bytes 18874372
  13.1 19.7 %copy-start.7 = (f32[2,256]{1,0:T(2,128)S(1)}, f32[2,256]{1,0:T(2,128)}, u32[]{:S(2)}) copy-start(f32[2,256]{1,0:T(2,128)} %param.6) | copy-start | bytes 6148
  25.4 77.0 %copy-start.5 = (bf16[1,2,96,96]{3,2,1,0:T(8,128)(2,1)S(1)}, bf16[1,2,96,96]{3,2,1,0:T(8,128)(2,1)}, u32[]{:S(2)}) copy-start(bf16[1,2,96,96]{3,2,1,0:T(8,128)(2,1)} %get-tuple-element.33) | copy-start | bytes 110596
  25.4 77.0 %copy-start.6 = (bf16[1,2,96,96]{3,2,1,0:T(8,128)(2,1)S(1)}, bf16[1,2,96,96]{3,2,1,0:T(8,128)(2,1)}, u32[]{:S(2)}) copy-start(bf16[1,2,96,96]{3,2,1,0:T(8,128)(2,1)} %get-tuple-element.34) | copy-start | bytes 110596
  32.9 1.0 copy-start.3
  34.0 1.0 copy-start.4
  100.6 1.7 %copy-start = (bf16[192,64,128]{2,1,0:T(8,128)(2,1)}, bf16[192,64,128]{2,1,0:T(8,128)(2,1)S(1)}, u32[]{:S(2)}) copy-start(bf16[192,64,128]{2,1,0:T(8,128)(2,1)S(1)} %exchange.1.g_ref) | copy-start | bytes 9437188
  103.6 1.9 %copy-start.1 = (bf16[192,64,128]{2,1,0:T(8,128)(2,1)S(1)}, bf16[192,64,128]{2,1,0:T(8,128)(2,1)}, u32[]{:S(2)}) copy-start(bf16[192,64,128]{2,1,0:T(8,128)(2,1)} %copy-done) | copy-start | bytes 9437188

commit v2 on v1

--- a/solution.py
+++ b/solution.py
@@ -237,15 +237,29 @@
         send(src, src, s_z.at[d - 1], r_z.at[d - 1], other(d)).wait_recv()
     held = gathered[...]
     cdev = held.shape[2]
-    cols = []
-    for j in range(part // 2):
-        cols.append(held[:, 2 * j : 2 * j + 2].reshape(nvar * 2 * cdev, LANES))
-    spectrum = jnp.concatenate(cols, 1)
-    hidden = jnp.dot(win_ref[...], spectrum, preferred_element_type=jnp.float32)
-    hidden = jnp.maximum(hidden + bias_ref[...], 0.0).astype(jnp.bfloat16)
-    mixed = jnp.dot(wout_ref[...], hidden, preferred_element_type=jnp.float32).astype(jnp.bfloat16)
-    for j in range(part // 2):
-        back[:, 2 * j : 2 * j + 2] = mixed[:, j * LANES : (j + 1) * LANES].reshape(nvar, 2, cdev, LANES)
+    real, imag = [
+        jnp.concatenate(
+            [held[:, 2 * j + q].reshape(nvar * cdev, LANES) for j in range(part // 2)], 1
+        )
+        for q in range(2)
+    ]
+
+    def product(a, b):
+        return jnp.dot(a, b, preferred_element_type=jnp.float32)
+
+    def mix(w_ref, a, b):
+        return (
+            product(w_ref[0], a) - product(w_ref[1], b),
+            product(w_ref[1], a) + product(w_ref[0], b),
+        )
+
+    pair_in = mix(win_ref, real, imag)
+    hidden = [jnp.maximum(pair_in[q] + bias_ref[q], 0.0).astype(jnp.bfloat16) for q in range(2)]
+    mixed = mix(wout_ref, *hidden)
+    for q in range(2):
+        for j in range(part // 2):
+            piece = mixed[q][:, j * LANES : (j + 1) * LANES].astype(jnp.bfloat16)
+            back[:, 2 * j + q] = piece.reshape(nvar, cdev, LANES)
     base = (lat * nlon + lon) * block
     bs = []
     for d in range(1, nvar):
@@ -339,11 +353,6 @@
         name="forward",
     )(state[0], etab, qtab)
 
-    hid = weights_in.shape[1]
-    win = complex_block(weights_in).reshape(2, hid, 2, nvar, cdev)
-    win = win.transpose(0, 1, 3, 2, 4).reshape(2 * hid, 2 * nvar * cdev)
-    wout = complex_block(weights_out).reshape(2, nvar, cdev, 2 * hid)
-    wout = wout.transpose(1, 0, 2, 3).reshape(2 * nvar * cdev, 2 * hid)
     chips = nlat * nlon // 2
     block = 2 * MLAT // (nlat * nlon)
     part = block // nvar
@@ -371,7 +380,7 @@
             collective_id=0, has_side_effects=True, vmem_limit_bytes=40 * 2**20
         ),
         name="exchange",
-    )(partial_value, win, bias_in.reshape(2 * hid, 1), wout)
+    )(partial_value, weights_in, bias_in[:, :, None], weights_out)
 
     rtab = lat_inverse(lat_first, latdev)
     rtab = rtab.transpose(0, 2, 3, 1).reshape(2 * latdev, 2 * MLAT)

time: 133 us -> 113 us (0.85)
  local copies, waits for them, and re-layouts: 26.2 us -> 9.12 us
  other arithmetic: 10 us -> 6.6 us
    reshape x2 -> x0, local copies, waits for them, and re-layouts: 7.41 us -> none  [kernel_body(): win = win.transpose(0, 1, 3, 2, 4).reshape(2 * hid, 2 * nvar * cdev)]
    another operation x4 -> x0, local copies, waits for them, and re-layouts: 4.88 us -> none  [the longest x2 2.93 us: complex_block(): jnp.stack([jnp.stack([real_part, -imag_part], 1), jnp.stack([imag_part, r...]
    transpose x2 -> x0, other arithmetic: 1.83 us -> none  [the longest x1 1 us: kernel_body(): wout = wout.transpose(1, 0, 2, 3).reshape(2 * nvar * cdev, 2 * hid)]
    slice x1 -> x0, local copies, waits for them, and re-layouts: 1.64 us -> none  [complex_block(): real_part, imag_part = (pair[0], pair[1])]
    unnamed x20 -> x12, local copies, waits for them, and re-layouts: 9.67 us -> 8.23 us
where the time goes in v2:
time: 113 us; the launch traced here: 112 us
  Pallas kernels  95 us (84%)
  local copies, waits for them, and re-layouts  9.12 us (8%)
  other arithmetic  6.6 us (6%)
  between operations  1.49 us (1%)
    pallas_call x1, Pallas kernels, kernel_body(): pl.pallas_call(functools.partial(exchange_kernel, sizes), in_specs=[vmem]...  65.6 us
    pallas_call x1, Pallas kernels, kernel_body(): pl.pallas_call(inverse_kernel, grid=(cdev // step,), in_specs=[pl.BlockSp...  14.5 us
    unnamed x12, local copies, waits for them, and re-layouts  8.23 us
    pallas_call x1, Pallas kernels, kernel_body(): pl.pallas_call(functools.partial(statistics_kernel, sizes), in_specs=[vme...  7.68 us
    pallas_call x1, Pallas kernels, kernel_body(): pl.pallas_call(forward_kernel, grid=(cdev // step,), in_specs=[pl.BlockSp...  7.19 us

profile of v2, /device:TPU:25, one launch (start us, length us, event | category | flops | bytes accessed | tf_op | source)
XLA Modules:
  0.0 112.2 jit_solution(15203700762172503974)
XLA Ops:
  0.7 0.5 negate_convert_fusion
  1.2 0.0 copy-start.5
  1.2 0.1 copy.17
  1.3 0.1 reshape.617.q_ref
  1.5 0.8 fusion.16
  2.3 0.1 copy.21.e_ref
  2.5 0.0 copy-start.2
  2.5 2.8 %copy-done.2 = bf16[1,64,96,512]{3,2,1,0:T(8,128)(2,1)S(1)} copy-done((bf16[1,64,96,512]{3,2,1,0:T(8,128)(2,1)S(1)}, bf16[1,64,96,512]{3,2,1,0:T(8,128)(2,1)}, u32[]{:S(2)}) %copy-start.2) | copy-done | bytes 6291480
  5.2 7.2 %forward.1.p_ref = bf16[192,64,128]{2,1,0:T(8,128)(2,1)S(1)} custom-call(bf16[64,96,512]{2,1,0:T(8,128)(2,1)S(1)} %bitcast.21, bf16[512,256]{1,0:T(8,128)(2,1)S(1)} %copy.21.e_ref, bf16[192,192]{1,0:T(8,128)(2,1)S(1)} %reshape.617.q_ref), custom_call_target="tpu_custom_call" | custom-call | tf_op jit(solution)/shard_map/forward/pallas_call | solution.py:342
  12.4 0.0 copy-start
  12.5 1.7 %copy-done = bf16[192,64,128]{2,1,0:T(8,128)(2,1)} copy-done((bf16[192,64,128]{2,1,0:T(8,128)(2,1)}, bf16[192,64,128]{2,1,0:T(8,128)(2,1)S(1)}, u32[]{:S(2)}) %copy-start) | copy-done | bytes 3145752
  14.1 0.0 copy-done.5
  14.1 0.1 copy.18.bias_ref
  14.3 0.0 copy-start.1
  14.3 1.9 %copy-done.1 = bf16[192,64,128]{2,1,0:T(8,128)(2,1)S(1)} copy-done((bf16[192,64,128]{2,1,0:T(8,128)(2,1)S(1)}, bf16[192,64,128]{2,1,0:T(8,128)(2,1)}, u32[]{:S(2)}) %copy-start.1) | copy-done | bytes 3145752
  16.2 0.0 copy-start.3
  16.2 0.9 copy-done.3
  17.1 0.0 copy-start.4
  17.1 0.9 copy-done.4
  18.1 65.6 %exchange.1.g_ref = bf16[192,64,128]{2,1,0:T(8,128)(2,1)S(1)} custom-call(bf16[192,64,128]{2,1,0:T(8,128)(2,1)S(1)} %copy-done.1, bf16[2,256,256]{2,1,0:T(8,128)(2,1)S(1)} %copy-done.3, f32[2,256,1]{2,1,0:T(8,128)S(1)} %copy.18.bias_ref, bf16[2,256,256]{2,1,0:T(8,128)(2,1)S(1)} %copy-done.4), custom_call_target="tpu_custom_call" | custom-call | tf_op jit(solution)/shard_map/exchange/pallas_call | solution.py:360
  83.7 0.1 copy.19
  83.8 0.1 reshape.618
  83.9 0.1 copy.20.r_ref
  84.0 0.8 multiply_convert_fusion.1
  84.9 14.5 %inverse.1 = (bf16[64,96,512]{2,1,0:T(8,128)(2,1)}, f32[64,96]{1,0:T(8,128)S(1)}, f32[64,96]{1,0:T(8,128)S(1)}) custom-call(bf16[192,64,128]{2,1,0:T(8,128)(2,1)S(1)} %exchange.1.g_ref, bf16[192,192]{1,0:T(8,128)(2,1)S(1)} %copy.20.r_ref, bf16[256,512]{1,0:T(8,128)(2,1)S(1)} %bitcast.22), custom_call_target="tpu_custom_call" | custom-call | tf_op jit(solution)/shard_map/inverse/pallas_call | solution.py:389
  99.4 0.1 multiply_reduce_fusion
  99.6 0.1 broadcast_in_dim.18
  99.6 0.7 pad_maximum_fusion.x_ref
  100.3 7.7 %statistics.1 = (f32[64,128]{1,0:T(8,128)}, f32[64,128]{1,0:T(8,128)}) custom-call(f32[64,128]{1,0:T(8,128)} %pad_maximum_fusion.x_ref), custom_call_target="tpu_custom_call" | custom-call | tf_op jit(solution)/shard_map/statistics/pallas_call | solution.py:415
  108.0 1.4 %multiply_bitcast_fusion = f32[1,64,96]{2,1,0:T(8,128)} fusion(f32[64,128]{1,0:T(8,128)} %get-tuple-element.11), kind=kLoop, calls=%fused_computation.58 | loop fusion | flops 6144 | bytes 49152 | tf_op jit(solution)/shard_map/div | solution.py:428
  109.4 0.6 cosine_reduce_fusion
  110.7 1.5 %fusion.31 = f32[64]{0:T(128)} fusion(f32[64,128]{1,0:T(8,128)} %get-tuple-element.12, f32[]{:T(128)S(6)} %mul.275), kind=kLoop, calls=%fused_computation.60 | loop fusion | flops 64 | bytes 516 | tf_op jit(solution)/shard_map/div | solution.py:428
  (11 shorter events, 0.2 us)
Async XLA Ops:
  1.2 13.0 %copy-start.5 = (f32[2,256]{1,0:T(2,128)S(1)}, f32[2,256]{1,0:T(2,128)}, u32[]{:S(2)}) copy-start(f32[2,256]{1,0:T(2,128)} %param.6) | copy-start | bytes 6148
  2.5 2.8 %copy-start.2 = (bf16[1,64,96,512]{3,2,1,0:T(8,128)(2,1)S(1)}, bf16[1,64,96,512]{3,2,1,0:T(8,128)(2,1)}, u32[]{:S(2)}) copy-start(bf16[1,64,96,512]{3,2,1,0:T(8,128)(2,1)} %param.4) | copy-start | bytes 18874372
  12.4 1.7 %copy-start = (bf16[192,64,128]{2,1,0:T(8,128)(2,1)}, bf16[192,64,128]{2,1,0:T(8,128)(2,1)S(1)}, u32[]{:S(2)}) copy-start(bf16[192,64,128]{2,1,0:T(8,128)(2,1)S(1)} %forward.1.p_ref) | copy-start | bytes 9437188
  14.3 1.9 %copy-start.1 = (bf16[192,64,128]{2,1,0:T(8,128)(2,1)S(1)}, bf16[192,64,128]{2,1,0:T(8,128)(2,1)}, u32[]{:S(2)}) copy-start(bf16[192,64,128]{2,1,0:T(8,128)(2,1)} %copy-done) | copy-start | bytes 9437188
  16.2 0.9 copy-start.3
  17.1 0.9 copy-start.4
